TPU v7x, 512 devices: a whole 4x8x8 slice. The times are simulated.
512 devices in a mesh: owner: 64 (over z, x, core), rep: 8 (over y).
Axes of the slice: x: 4, y: 8, z: 8, core: 2. Of those that a mesh axis runs over, the one named last changes fastest.
Arguments:
- features: float32 [262144, 256], P(('owner', 'rep')), may hold values from -6 to 6
- group_ids: int32 [262144], P(('owner', 'rep')), may hold values from 0 to 65535, as said below
- survive: int32 [262144], P(('owner', 'rep')), may hold values from 0 to 1
- home_row: int32 [65536], replicated, may hold values from 0 to 65535, as said below
- hot_ids: int32 [256], replicated, may hold values from 0 to 65535, as said below
Outputs:
- group_out: float32 [65536, 256], P(('owner', 'rep'))
- group_count: float32 [65536], P(('owner', 'rep'))
- hot_out: float32 [256, 256], P('rep')
- hot_count: float32 [256], P('rep')
Inputs may be any that keep to these rules, and one draw needn't show every extreme that they name: home_row is a permutation of the groups. hot_ids holds 256 different groups. `group_ids`: among the rows of one device, 128 name hot groups, and at most 16 rows name non-hot groups g whose home_row[g] // 1024 is one and the same owner index; on every device some owners get exactly 16 such rows.
All inputs are finite; a program needn't handle non-finite values.
Results may differ from a plain program's by a relative error of at most 0.00007.
Values sent between devices are 32-bit elements; how exact they have to be, the bound alone decides.
A program may use at most 64 MiB of HBM per device.

v0:
```python
import math
import jax
import jax.numpy as jnp
from jax import lax
from jax.sharding import Mesh
from jax.sharding import PartitionSpec as P

OWNER = ("owner_0", "owner_1", "owner_2")
OWNER_REP = ("owner_0", "owner_1", "owner_2", "rep")


def split_up(shard, dim, devices):
    before, after = (shard.shape[:dim], shard.shape[dim + 1 :])
    return jnp.moveaxis(shard.reshape(*before, devices, -1, *after), dim, 0)


def sent_and_summed(shard, axis, dim):
    devices = lax.axis_size(axis)
    parts = lax.all_to_all(split_up(shard, dim, devices), axis, 0, 0, tiled=True)
    return jnp.sum(parts, axis=0)


def in_one_piece(arrays, axis, dim, along):
    columns = [a.reshape(*a.shape[:along], -1) for a in arrays]
    both = jnp.concatenate(columns, axis=along)
    out, at, done = (sent_and_summed(both, axis, dim), 0, [])
    for a, column in zip(arrays, columns):
        slab = out[..., at : at + column.shape[along]]
        done.append(slab.reshape(*slab.shape[:along], *a.shape[along:]))
        at += column.shape[along]
    return tuple(done)


def one_axis_at_a_time(shard, axes):
    for axis in axes:
        shard = lax.psum(shard, axis)
    return shard


def sent_together(arrays, axis, split_dim, concat_dim, along):
    widths = [math.prod(a.shape[along:]) for a in arrays]
    both = jnp.concatenate(
        [a.reshape(*a.shape[:along], w) for a, w in zip(arrays, widths)], axis=along
    )
    out = lax.all_to_all(both, axis, split_axis=split_dim, concat_axis=concat_dim, tiled=True)
    parts = jnp.split(out, [sum(widths[:k]) for k in range(1, len(widths))], axis=along)
    return tuple((b.reshape(*out.shape[:along], *a.shape[along:]) for a, b in zip(arrays, parts)))


def local(features, group_ids, survive, home_row, hot_ids):
    rows = features.shape[0]
    width = features.shape[1]
    owners = lax.axis_size(OWNER)
    own_groups = home_row.shape[0] // owners
    capacity = 2 * rows // owners
    live = survive == 1
    matches = group_ids[:, None] == hot_ids[None, :]
    is_hot = jnp.any(matches, axis=1)
    hot_table = jnp.where(matches & live[:, None], 1.0, 0.0).astype(jnp.float32)
    hot_part = lax.dot_general(
        hot_table,
        features,
        (((0,), (0,)), ((), ())),
        precision=lax.Precision.HIGHEST,
        preferred_element_type=jnp.float32,
    )
    hot_tally = jnp.sum(hot_table, axis=0)
    part_sum, part_tally = in_one_piece((hot_part, hot_tally), "rep", 0, 1)
    hot_sum, hot_count = (
        one_axis_at_a_time(part_sum, OWNER),
        one_axis_at_a_time(part_tally, OWNER),
    )
    hot_out = hot_sum / jnp.sqrt(1.0 + hot_count)[:, None]
    keep = live & jnp.logical_not(is_hot)
    destination = home_row[group_ids]
    target = destination // own_groups
    local_row = (destination % own_groups).astype(jnp.float32)
    member = (
        (target[:, None] == jnp.arange(owners, dtype=jnp.int32)[None, :]) & keep[:, None]
    ).astype(jnp.int32)
    position = jnp.cumsum(member, axis=0) - 1
    placed = jnp.sum(position * member, axis=1)
    target_safe = jnp.where(keep, target, owners)
    placed_safe = jnp.where(keep, placed, 0)
    bucket = (
        jnp.zeros((owners, capacity, width), jnp.float32)
        .at[target_safe, placed_safe]
        .set(features, mode="drop")
    )
    labels = (
        jnp.full((owners, capacity), -1.0, jnp.float32)
        .at[target_safe, placed_safe]
        .set(local_row, mode="drop")
    )
    arrived, arrived_labels = sent_together((bucket, labels), OWNER, 0, 0, 2)
    total_rows = owners * capacity
    block = min(512, total_rows)
    flat_rows = arrived.reshape(total_rows // block, block, width)
    flat_labels = arrived_labels.astype(jnp.int32).reshape(total_rows // block, block)
    columns = jnp.arange(own_groups, dtype=jnp.int32)

    def add_block(carry, item):
        total, tally = carry
        block_rows, block_labels = item
        onehot = (block_labels[:, None] == columns[None, :]).astype(jnp.float32)
        total = total + lax.dot_general(
            onehot,
            block_rows,
            (((0,), (0,)), ((), ())),
            precision=lax.Precision.HIGHEST,
            preferred_element_type=jnp.float32,
        )
        tally = tally + jnp.sum(onehot, axis=0)
        return ((total, tally), None)

    start_carry = (
        jnp.zeros((own_groups, width), jnp.float32),
        jnp.zeros((own_groups,), jnp.float32),
    )
    (dense, dense_tally), _ = lax.scan(add_block, start_carry, (flat_rows, flat_labels))
    cold_sum, group_count = in_one_piece((dense, dense_tally), "rep", 0, 1)
    group_out = cold_sum / jnp.sqrt(1.0 + group_count)[:, None]
    return (group_out, group_count, hot_out, hot_count)


def solution(mesh):
    split = Mesh(
        mesh.devices.reshape(8, 4, 2, mesh.shape["rep"]), ("owner_0", "owner_1", "owner_2", "rep")
    )
    return jax.shard_map(
        local,
        mesh=split,
        in_specs=(P(OWNER_REP, None), P(OWNER_REP), P(OWNER_REP), P(), P()),
        out_specs=(P(OWNER_REP, None), P(OWNER_REP), P("rep", None), P("rep")),
        check_vma=False,
    )
```

profile of v0, /device:TPU:1, one launch (start us, length us, event | category | flops | bytes accessed | tf_op | source)
XLA Modules:
  0.0 193.5 jit_solution(14835666861502887366)
XLA Ops:
  0.6 0.0 copy-start
  0.6 0.0 copy-start.5
  0.7 0.7 compare_select_fusion.2
  1.4 0.9 compare_reduce_fusion
  2.3 3.1 %gather_fusion = s32[512]{0:T(512)S(1)} fusion(s32[65536]{0:T(1024)S(1)} %copy-done, s32[1024]{0:T(1024)S(1)} %pad_clamp_fusion), kind=kCustom, calls=%fused_computation | custom fusion | bytes 6144 | tf_op jit(solution)/shard_map/gather | solution.py:75
  5.5 0.0 copy-done.5
  5.6 1.2 reduce-window.6
  6.8 0.2 slice_reduce_fusion
  7.0 0.1 fusion.19
  7.2 25.2 %scatter_fusion.1 = f32[64,16]{0,1:T(8,128)S(1)} fusion(f32[64,16]{0,1:T(8,128)S(1)} %broadcast_in_dim.53, s32[512]{0:T(512)S(1)} %bitcast.56, f32[512]{0:T(512)S(1)} %get-tuple-element.89), kind=kCustom, calls=%fused_computation.2 | custom fusion | bytes 10240 | tf_op jit(solution)/shard_map/scatter | solution.py:93
  32.4 0.0 copy-start.2
  32.4 0.3 copy.34
  32.7 0.1 broadcast_in_dim.48
  32.9 0.6 copy-done.2
  33.5 26.3 %scatter_fusion = f32[64,16,256]{2,1,0:T(8,128)S(1)} fusion(f32[64,16,256]{2,1,0:T(8,128)S(1)} %broadcast_in_dim.48, s32[512]{0:T(512)S(1)} %bitcast.57, f32[512,256]{1,0:T(8,128)S(1)} %copy-done.2), kind=kCustom, calls=%fused_computation.1 | custom fusion | bytes 1576960 | tf_op jit(solution)/shard_map/scatter | solution.py:88
  59.8 1.3 pad_maximum_fusion
  61.1 14.9 %all-to-all-start = ((f32[64,16,257]{2,1,0:T(8,128)}), f32[64,16,257]{2,1,0:T(8,128)S(1)}, u32[]{:S(2)}, u32[]{:S(2)}) async-start(f32[64,16,257]{2,1,0:T(8,128)} %pad_maximum_fusion), calls=%async_computation | async-start | bytes 3145728 | tf_op jit(solution)/shard_map/all_to_all | solution.py:45
  76.0 0.8 select_reduce_fusion
  76.8 0.9 concatenate.35
  77.7 1.0 fusion.10
  78.7 0.8 pad_maximum_fusion.2
  79.4 35.6 %all-to-all-done = f32[64,16,257]{2,1,0:T(8,128)S(1)} async-done(((f32[64,16,257]{2,1,0:T(8,128)}), f32[64,16,257]{2,1,0:T(8,128)S(1)}, u32[]{:S(2)}, u32[]{:S(2)}) %all-to-all-start) | async-done | bytes 1052704 | tf_op jit(solution)/shard_map/all_to_all | solution.py:45
  115.1 6.8 %all-to-all-start.2 = ((f32[8,32,257]{2,1,0:T(8,128)}), f32[8,32,257]{2,1,0:T(8,128)}, u32[]{:S(2)}, u32[]{:S(2)}) async-start(f32[8,32,257]{2,1,0:T(8,128)} %pad_maximum_fusion.2), calls=%async_computation.2 | async-start | bytes 786432 | tf_op jit(solution)/shard_map/all_to_all | solution.py:19
  121.9 1.2 fusion.12
  123.0 0.0 copy-done.1
  123.0 0.1 convert_element_type.21
  123.1 1.3 split.9
  124.4 5.0 %while.13 = (s32[]{:T(128)}, f32[1024,256]{1,0:T(8,128)S(1)}, f32[1024]{0:T(1024)S(1)}, s32[2,512]{1,0:T(2,128)S(1)}, f32[2,512,256]{2,1,0:T(8,128)S(1)}, /*index=5*/s32[]{:T(128)}, s32[]{:T(128)}) while((s32[]{:T(128)}, f32[1024,256]{1,0:T(8,128)S(1)}, f32[1024]{0:T(1024)S(1)}, s32[2,512]{1,0:T(2,128)S(1)}, ...), condition=%wide.region_8.9_spmd.clone, body=%wide.region_6.0_spmd.clone.sunk | while | flops 1613235200 | bytes 2646120 | solution.py:120
  124.5 0.3 fusion.37
  124.7 2.2 %fusion.36 = f32[1024,256]{1,0:T(8,128)S(1)} fusion(f32[1024,256]{1,0:T(8,128)S(1)} %get-tuple-element.129, s32[512]{0:T(512)S(1)} %bitcast.62, f32[2,512,256]{2,1,0:T(8,128)S(1)} %get-tuple-element.139, s32[]{:T(128)S(6)} %copy.46, pred[]{:T(512)S(6)} %compare.22), kind=kOutput, calls=%fused_computation.8.clone.1 | convolution fusion | flops 1611661312 | bytes 2623493 | tf_op jit(solution)/shard_map/while/body/eval_jaxpr/dot_general | solution.py:106
  126.9 0.3 fusion.37
  127.2 2.2 %fusion.36 = f32[1024,256]{1,0:T(8,128)S(1)} fusion(f32[1024,256]{1,0:T(8,128)S(1)} %get-tuple-element.129, s32[512]{0:T(512)S(1)} %bitcast.62, f32[2,512,256]{2,1,0:T(8,128)S(1)} %get-tuple-element.139, s32[]{:T(128)S(6)} %copy.46, pred[]{:T(512)S(6)} %compare.22), kind=kOutput, calls=%fused_computation.8.clone.1 | convolution fusion | flops 1611661312 | bytes 2623493 | tf_op jit(solution)/shard_map/while/body/eval_jaxpr/dot_general | solution.py:106
  129.4 0.2 copy.35
  129.6 0.1 pad_maximum_fusion.1
  129.8 1.5 copy.36
  131.2 3.3 %all-to-all-done.2 = f32[8,32,257]{2,1,0:T(8,128)} async-done(((f32[8,32,257]{2,1,0:T(8,128)}), f32[8,32,257]{2,1,0:T(8,128)}, u32[]{:S(2)}, u32[]{:S(2)}) %all-to-all-start.2) | async-done | bytes 263200 | tf_op jit(solution)/shard_map/all_to_all | solution.py:19
  134.5 3.6 %all-to-all-start.1 = ((f32[8,128,257]{1,2,0:T(8,128)}), f32[8,128,257]{1,2,0:T(8,128)S(1)}, u32[]{:S(2)}, u32[]{:S(2)}) async-start(f32[8,128,257]{1,2,0:T(8,128)} %copy.36), calls=%async_computation.1 | async-start | bytes 2162688 | tf_op jit(solution)/shard_map/all_to_all | solution.py:19
  138.1 1.0 reduce_sum.48
  139.1 0.1 slice_reduce_fusion.1
  139.2 26.8 %all-reduce = (f32[32,256]{1,0:T(8,128)S(1)}, f32[32]{0:T(128)S(1)}) all-reduce(f32[32,256]{1,0:T(8,128)S(1)} %slice.33, f32[32]{0:T(128)S(1)} %slice_reduce_fusion.1), channel_id=1, replica_groups=mesh['owner_0'=8,'owner_1'=4,'owner_2'=2,'rep'=8] {'owner_0'}, use_global_device_ids=true, to_apply=%region_12.13 | all-reduce | flops 8224 | bytes 65792 | tf_op jit(solution)/shard_map/psum | solution.py:36
  166.0 11.9 %all-reduce.1 = (f32[32,256]{1,0:T(8,128)S(1)}, f32[32]{0:T(128)S(1)}) all-reduce(f32[32,256]{1,0:T(8,128)S(1)} %get-tuple-element.77, f32[32]{0:T(128)S(1)} %get-tuple-element.78), channel_id=1, replica_groups=mesh['owner_0'=8,'owner_1'=4,'owner_2'=2,'rep'=8] {'owner_1'}, use_global_device_ids=true, to_apply=%region_13.14 | all-reduce | flops 8224 | bytes 65792 | tf_op jit(solution)/shard_map/psum | solution.py:36
  177.9 13.6 %all-reduce.2 = (f32[32,256]{1,0:T(8,128)S(1)}, f32[32]{0:T(128)S(1)}) all-reduce(f32[32,256]{1,0:T(8,128)S(1)} %get-tuple-element.79, f32[32]{0:T(128)S(1)} %get-tuple-element.80), channel_id=1, replica_groups=mesh['owner_0'=8,'owner_1'=4,'owner_2'=2,'rep'=8] {'owner_2'}, use_global_device_ids=true, to_apply=%region_14.15 | all-reduce | flops 8224 | bytes 65792 | tf_op jit(solution)/shard_map/psum | solution.py:36
  191.4 0.0 copy-start.6
  191.5 0.7 broadcast_divide_fusion
  192.2 0.0 all-to-all-done.1
  192.2 0.1 reduce_sum.46
  192.2 0.5 slice_bitcast_fusion
  192.8 0.8 copy.38
  (25 shorter events, 0.2 us)
Async XLA Ops:
  0.6 1.7 copy-start
  0.6 4.9 %copy-start.5 = (s32[512]{0:T(512)S(1)}, s32[512]{0:T(512)}, u32[]{:S(2)}) copy-start(s32[512]{0:T(512)} %param.9) | copy-start | bytes 6148
  32.4 1.0 copy-start.2
  61.1 14.9 %copy-start.3 = (s32[512]{0:T(512)S(1)}, s32[512]{0:T(512)}, u32[]{:S(2)}) copy-start(s32[512]{0:T(512)} %param.8) | copy-start | bytes 6148
  61.1 15.0 %copy-start.4 = (s32[256]{0:T(256)S(1)}, s32[256]{0:T(256)}, u32[]{:S(2)}) copy-start(s32[256]{0:T(256)} %param.11) | copy-start | bytes 3076
  61.1 54.0 %all-to-all-start = ((f32[64,16,257]{2,1,0:T(8,128)}), f32[64,16,257]{2,1,0:T(8,128)S(1)}, u32[]{:S(2)}, u32[]{:S(2)}) async-start(f32[64,16,257]{2,1,0:T(8,128)} %pad_maximum_fusion), calls=%async_computation | async-start | bytes 3145728 | tf_op jit(solution)/shard_map/all_to_all | solution.py:45
  115.1 8.0 %copy-start.1 = (f32[64,16,257]{2,1,0:T(8,128)}, f32[64,16,257]{2,1,0:T(8,128)S(1)}, u32[]{:S(2)}) copy-start(f32[64,16,257]{2,1,0:T(8,128)S(1)} %all-to-all-done) | copy-start | bytes 3158020
  115.1 19.4 %all-to-all-start.2 = ((f32[8,32,257]{2,1,0:T(8,128)}), f32[8,32,257]{2,1,0:T(8,128)}, u32[]{:S(2)}, u32[]{:S(2)}) async-start(f32[8,32,257]{2,1,0:T(8,128)} %pad_maximum_fusion.2), calls=%async_computation.2 | async-start | bytes 786432 | tf_op jit(solution)/shard_map/all_to_all | solution.py:19
  134.5 57.7 %all-to-all-start.1 = ((f32[8,128,257]{1,2,0:T(8,128)}), f32[8,128,257]{1,2,0:T(8,128)S(1)}, u32[]{:S(2)}, u32[]{:S(2)}) async-start(f32[8,128,257]{1,2,0:T(8,128)} %copy.36), calls=%async_computation.1 | async-start | bytes 2162688 | tf_op jit(solution)/shard_map/all_to_all | solution.py:19
  191.4 2.1 %copy-start.6 = (f32[32]{0:T(128)}, f32[32]{0:T(128)S(1)}, u32[]{:S(2)}) copy-start(f32[32]{0:T(128)S(1)} %get-tuple-element.82) | copy-start | bytes 388
where the time goes:
time: 194 us
  local copies, waits for them, and re-layouts  60.8 us (31%)
  blocking collectives  52.2 us (27%)
  waiting for transfers between devices  38.9 us (20%)
  starting transfers between devices  25.3 us (13%)
  other arithmetic  10.1 us (5%)
  matrix products  5.27 us (3%)
    psum x3, blocking collectives, one_axis_at_a_time(): shard = lax.psum(shard, axis)  52.2 us
    all_to_all x1, waiting for transfers between devices, sent_together(): lax.all_to_all(both, axis, split_axis=split_dim, concat_axis=concat_dim,...  35.6 us
    scatter x1, local copies, waits for them, and re-layouts, local(): bucket = jnp.zeros((owners, capacity, width), jnp.float32).at[target_safe...  26.3 us
    scatter x1, local copies, waits for them, and re-layouts, local(): labels = jnp.full((owners, capacity), -1.0, jnp.float32).at[target_safe,...  25.2 us
    all_to_all x1, starting transfers between devices, sent_together(): lax.all_to_all(both, axis, split_axis=split_dim, concat_axis=concat_dim,...  14.9 us
    all_to_all x2, starting transfers between devices, sent_and_summed(): lax.all_to_all(split_up(shard, dim, devices), axis, 0, 0, tiled=True)  10.4 us
    dot_general x2, matrix products, add_block(): lax.dot_general(onehot, block_rows, (((0,), (0,)), ((), ())), precision=l...  4.31 us
  transfers between devices with their start and end apart: 3, of which 2 were waited for; matrix products, arithmetic and copies ran while one was open for 7% of the time, Pallas kernels for 0%

commit v1 on v0

--- a/solution.py
+++ b/solution.py
@@ -33,7 +33,7 @@
 
 def one_axis_at_a_time(shard, axes):
     for axis in axes:
-        shard = lax.psum(shard, axis)
+        shard = jnp.sum(lax.all_gather(shard, axis), axis=0)
     return shard
 
 

time: 194 us -> 219 us (1.13)
  blocking collectives: 52.2 us -> 69.7 us
  local copies, waits for them, and re-layouts: 60.8 us -> 65.6 us
    psum x3 -> x0, blocking collectives: 52.2 us -> none  [one_axis_at_a_time(): shard = lax.psum(shard, axis)]
    all_gather x0 -> x3, blocking collectives: none -> 38.6 us  [one_axis_at_a_time(): shard = jnp.sum(lax.all_gather(shard, axis), axis=0)]
    unnamed x0 -> x3, blocking collectives: none -> 31.1 us
    unnamed x15 -> x24, local copies, waits for them, and re-layouts: 1.38 us -> 5.91 us
  transfers between devices with their start and end apart: 3 -> 3, of which waited for: 2 -> 2; matrix products, arithmetic and copies ran while one was open for 7% -> 9% of each run, Pallas kernels for 0% -> 0%
where the time goes in v1:
time: 219 us; the launch traced here: 218 us
  blocking collectives  69.7 us (32%)
  local copies, waits for them, and re-layouts  65.6 us (30%)
  waiting for transfers between devices  38.9 us (18%)
  starting transfers between devices  25.3 us (12%)
  other arithmetic  10.2 us (5%)
  matrix products  5.26 us (2%)
  between operations  2.86 us (1%)
    all_gather x3, blocking collectives, one_axis_at_a_time(): shard = jnp.sum(lax.all_gather(shard, axis), axis=0)  38.6 us
    all_to_all x1, waiting for transfers between devices, sent_together(): lax.all_to_all(both, axis, split_axis=split_dim, concat_axis=concat_dim,...  35.6 us
    unnamed x3, blocking collectives  31.1 us
    scatter x1, local copies, waits for them, and re-layouts, local(): bucket = jnp.zeros((owners, capacity, width), jnp.float32).at[target_safe...  26.3 us
    scatter x1, local copies, waits for them, and re-layouts, local(): labels = jnp.full((owners, capacity), -1.0, jnp.float32).at[target_safe,...  25.2 us
    all_to_all x1, starting transfers between devices, sent_together(): lax.all_to_all(both, axis, split_axis=split_dim, concat_axis=concat_dim,...  14.9 us
    all_to_all x2, starting transfers between devices, sent_and_summed(): lax.all_to_all(split_up(shard, dim, devices), axis, 0, 0, tiled=True)  10.4 us
    unnamed x24, local copies, waits for them, and re-layouts  5.91 us
  transfers between devices with their start and end apart: 3, of which 2 were waited for; matrix products, arithmetic and copies ran while one was open for 9% of the time, Pallas kernels for 0%

profile of v1, /device:TPU:1, one launch (start us, length us, event | category | flops | bytes accessed | tf_op | source)
XLA Modules:
  0.0 217.9 jit_solution(9582196979197142040)
XLA Ops:
  0.7 0.7 compare_select_fusion.2
  1.4 0.9 compare_reduce_fusion
  2.3 3.1 %gather_fusion = s32[512]{0:T(512)S(1)} fusion(s32[65536]{0:T(1024)S(1)} %copy-done, s32[1024]{0:T(1024)S(1)} %pad_clamp_fusion), kind=kCustom, calls=%fused_computation | custom fusion | bytes 6144 | tf_op jit(solution)/shard_map/gather | solution.py:75
  5.6 1.2 reduce-window.6
  6.8 0.2 slice_reduce_fusion
  7.0 0.1 fusion.19
  7.2 25.2 %scatter_fusion.1 = f32[64,16]{0,1:T(8,128)S(1)} fusion(f32[64,16]{0,1:T(8,128)S(1)} %broadcast_in_dim.53, s32[512]{0:T(512)S(1)} %bitcast.60, f32[512]{0:T(512)S(1)} %get-tuple-element.83), kind=kCustom, calls=%fused_computation.2 | custom fusion | bytes 10240 | tf_op jit(solution)/shard_map/scatter | solution.py:93
  32.4 0.3 copy.34
  32.7 0.1 broadcast_in_dim.48
  32.9 0.6 copy-done.2
  33.4 26.3 %scatter_fusion = f32[64,16,256]{2,1,0:T(8,128)S(1)} fusion(f32[64,16,256]{2,1,0:T(8,128)S(1)} %broadcast_in_dim.48, s32[512]{0:T(512)S(1)} %bitcast.61, f32[512,256]{1,0:T(8,128)S(1)} %copy-done.2), kind=kCustom, calls=%fused_computation.1 | custom fusion | bytes 1576960 | tf_op jit(solution)/shard_map/scatter | solution.py:88
  59.8 1.3 pad_maximum_fusion
  61.1 14.9 %all-to-all-start = ((f32[64,16,257]{2,1,0:T(8,128)}), f32[64,16,257]{2,1,0:T(8,128)S(1)}, u32[]{:S(2)}, u32[]{:S(2)}) async-start(f32[64,16,257]{2,1,0:T(8,128)} %pad_maximum_fusion), calls=%async_computation | async-start | bytes 3145728 | tf_op jit(solution)/shard_map/all_to_all | solution.py:45
  76.0 0.8 select_reduce_fusion
  76.8 0.9 concatenate.35
  77.7 1.0 fusion.10
  78.7 0.8 pad_maximum_fusion.2
  79.4 35.6 %all-to-all-done = f32[64,16,257]{2,1,0:T(8,128)S(1)} async-done(((f32[64,16,257]{2,1,0:T(8,128)}), f32[64,16,257]{2,1,0:T(8,128)S(1)}, u32[]{:S(2)}, u32[]{:S(2)}) %all-to-all-start) | async-done | bytes 1052704 | tf_op jit(solution)/shard_map/all_to_all | solution.py:45
  115.1 6.8 %all-to-all-start.2 = ((f32[8,32,257]{2,1,0:T(8,128)}), f32[8,32,257]{2,1,0:T(8,128)}, u32[]{:S(2)}, u32[]{:S(2)}) async-start(f32[8,32,257]{2,1,0:T(8,128)} %pad_maximum_fusion.2), calls=%async_computation.2 | async-start | bytes 786432 | tf_op jit(solution)/shard_map/all_to_all | solution.py:19
  121.9 1.2 fusion.12
  123.1 1.3 split.9
  124.4 5.0 %while.13 = (s32[]{:T(128)}, f32[1024,256]{1,0:T(8,128)S(1)}, f32[1024]{0:T(1024)S(1)}, s32[2,512]{1,0:T(2,128)S(1)}, f32[2,512,256]{2,1,0:T(8,128)S(1)}, /*index=5*/s32[]{:T(128)}, s32[]{:T(128)}) while((s32[]{:T(128)}, f32[1024,256]{1,0:T(8,128)S(1)}, f32[1024]{0:T(1024)S(1)}, s32[2,512]{1,0:T(2,128)S(1)}, ...), condition=%wide.region_8.9_spmd.clone, body=%wide.region_6.0_spmd.clone.sunk | while | flops 1613235200 | bytes 2646112 | solution.py:120
  124.4 2.1 fusion.36
  126.6 0.3 fusion.37
  126.9 2.2 fusion.36
  129.1 0.3 fusion.37
  129.4 0.2 copy.35
  129.6 0.1 pad_maximum_fusion.1
  129.8 1.5 copy.36
  131.2 3.3 %all-to-all-done.2 = f32[8,32,257]{2,1,0:T(8,128)} async-done(((f32[8,32,257]{2,1,0:T(8,128)}), f32[8,32,257]{2,1,0:T(8,128)}, u32[]{:S(2)}, u32[]{:S(2)}) %all-to-all-start.2) | async-done | bytes 263200 | tf_op jit(solution)/shard_map/all_to_all | solution.py:19
  134.5 3.6 %all-to-all-start.1 = ((f32[8,128,257]{1,2,0:T(8,128)}), f32[8,128,257]{1,2,0:T(8,128)S(1)}, u32[]{:S(2)}, u32[]{:S(2)}) async-start(f32[8,128,257]{1,2,0:T(8,128)} %copy.36), calls=%async_computation.1 | async-start | bytes 2162688 | tf_op jit(solution)/shard_map/all_to_all | solution.py:19
  138.1 1.3 dynamic-slice
  139.3 1.3 dynamic-slice.1
  141.9 1.3 dynamic-slice.2
  143.8 1.0 reduce_sum.102
  144.9 0.1 slice_reduce_fusion.1
  145.0 0.2 dynamic-update-slice
  145.2 16.1 %all-reduce = f32[256]{0:T(256)S(1)} all-reduce(f32[256]{0:T(256)S(1)} %dynamic-update-slice), channel_id=5, replica_groups=mesh['owner_0'=8,'owner_1'=4,'owner_2'=2,'rep'=8] {'owner_0'}, use_global_device_ids=true, to_apply=%add | all-reduce | flops 256 | bytes 2048
  161.4 0.2 dynamic-update-slice.1
  161.6 7.0 %all-reduce.1 = f32[128]{0:T(128)S(1)} all-reduce(f32[128]{0:T(128)S(1)} %dynamic-update-slice.1), channel_id=6, replica_groups=mesh['owner_0'=8,'owner_1'=4,'owner_2'=2,'rep'=8] {'owner_1'}, use_global_device_ids=true, to_apply=%add.1 | all-reduce | flops 128 | bytes 1024
  168.7 0.2 dynamic-update-slice.2
  169.0 8.0 %all-reduce.2 = f32[64]{0:T(128)S(1)} all-reduce(f32[64]{0:T(128)S(1)} %dynamic-update-slice.2), channel_id=7, replica_groups=mesh['owner_0'=8,'owner_1'=4,'owner_2'=2,'rep'=8] {'owner_2'}, use_global_device_ids=true, to_apply=%add.2 | all-reduce | flops 64 | bytes 512
  177.1 18.4 %all-gather = f32[256,256]{1,0:T(8,128)S(1)} all-gather(f32[32,256]{1,0:T(8,128)S(1)} %slice.33), channel_id=2, replica_groups=mesh['owner_0'=8,'owner_1'=4,'owner_2'=2,'rep'=8] {'owner_0'}, dimensions={0}, use_global_device_ids=true | all-gather | bytes 294912 | tf_op jit(solution)/shard_map/all_gather | solution.py:36
  195.6 9.1 %all-gather.1 = f32[128,256]{1,0:T(8,128)S(1)} all-gather(f32[32,256]{1,0:T(8,128)S(1)} %reduce_sum.103), channel_id=3, replica_groups=mesh['owner_0'=8,'owner_1'=4,'owner_2'=2,'rep'=8] {'owner_1'}, dimensions={0}, use_global_device_ids=true | all-gather | bytes 163840 | tf_op jit(solution)/shard_map/all_gather | solution.py:36
  204.7 11.1 %all-gather.2 = f32[64,256]{1,0:T(8,128)S(1)} all-gather(f32[32,256]{1,0:T(8,128)S(1)} %reduce_sum.104), channel_id=4, replica_groups=mesh['owner_0'=8,'owner_1'=4,'owner_2'=2,'rep'=8] {'owner_2'}, dimensions={0}, use_global_device_ids=true | all-gather | bytes 98304 | tf_op jit(solution)/shard_map/all_gather | solution.py:36
  215.8 0.7 broadcast_divide_fusion
  216.6 0.5 slice_bitcast_fusion
  217.1 0.8 copy.38
  (46 shorter events, 0.7 us)
Async XLA Ops:
  0.6 1.7 copy-start
  0.6 4.9 %copy-start.5 = (s32[512]{0:T(512)S(1)}, s32[512]{0:T(512)}, u32[]{:S(2)}) copy-start(s32[512]{0:T(512)} %param.9) | copy-start | bytes 6148
  32.4 1.0 copy-start.2
  61.1 14.9 %copy-start.3 = (s32[512]{0:T(512)S(1)}, s32[512]{0:T(512)}, u32[]{:S(2)}) copy-start(s32[512]{0:T(512)} %param.8) | copy-start | bytes 6148
  61.1 15.0 %copy-start.4 = (s32[256]{0:T(256)S(1)}, s32[256]{0:T(256)}, u32[]{:S(2)}) copy-start(s32[256]{0:T(256)} %param.11) | copy-start | bytes 3076
  61.1 54.0 %all-to-all-start = ((f32[64,16,257]{2,1,0:T(8,128)}), f32[64,16,257]{2,1,0:T(8,128)S(1)}, u32[]{:S(2)}, u32[]{:S(2)}) async-start(f32[64,16,257]{2,1,0:T(8,128)} %pad_maximum_fusion), calls=%async_computation | async-start | bytes 3145728 | tf_op jit(solution)/shard_map/all_to_all | solution.py:45
  115.1 8.0 %copy-start.1 = (f32[64,16,257]{2,1,0:T(8,128)}, f32[64,16,257]{2,1,0:T(8,128)S(1)}, u32[]{:S(2)}) copy-start(f32[64,16,257]{2,1,0:T(8,128)S(1)} %all-to-all-done) | copy-start | bytes 3158020
  115.1 19.4 %all-to-all-start.2 = ((f32[8,32,257]{2,1,0:T(8,128)}), f32[8,32,257]{2,1,0:T(8,128)}, u32[]{:S(2)}, u32[]{:S(2)}) async-start(f32[8,32,257]{2,1,0:T(8,128)} %pad_maximum_fusion.2), calls=%async_computation.2 | async-start | bytes 786432 | tf_op jit(solution)/shard_map/all_to_all | solution.py:19
  134.5 82.0 %all-to-all-start.1 = ((f32[8,128,257]{1,2,0:T(8,128)}), f32[8,128,257]{1,2,0:T(8,128)S(1)}, u32[]{:S(2)}, u32[]{:S(2)}) async-start(f32[8,128,257]{1,2,0:T(8,128)} %copy.36), calls=%async_computation.1 | async-start | bytes 2162688 | tf_op jit(solution)/shard_map/all_to_all | solution.py:19
  177.1 40.8 %copy-start.6 = (f32[32]{0:T(128)}, f32[32]{0:T(128)S(1)}, u32[]{:S(2)}) copy-start(f32[32]{0:T(128)S(1)} %reduce_sum.108) | copy-start | bytes 388
